TPU v7x, 32 devices: a whole 2x2x4 slice. The times are simulated.
32 devices in a mesh: grp: 2 (over y), kvp: 4 (over z), tp: 4 (over x, core).
Axes of the slice: x: 2, y: 2, z: 4, core: 2. Of those that a mesh axis runs over, the one named last changes fastest.
Arguments:
- queries: bfloat16 [32, 4096], P('grp', 'tp'), parts along dimension 0, may hold values from -6 to 6
- keys: bfloat16 [32, 512, 512], P('grp', 'kvp', 'tp'), parts along dimension 0, may hold values from -6 to 6
- values: bfloat16 [32, 512, 512], P('grp', 'kvp', 'tp'), parts along dimension 0, may hold values from -6 to 6
- lengths: int32 [32], P('grp'), parts along dimension 0, may hold values from 256 to 512, as said below
- out_weight: bfloat16 [4096, 1536], P('tp', 'kvp'), may hold values from -0.375 to 0.375
- residual: bfloat16 [32, 1536], P('grp', 'kvp'), parts along dimension 0, may hold values from -20 to 20
- norm_gain: bfloat16 [1536], P('kvp'), may hold values from 0.099609375 to 1.8984375
- expert_ids: int32 [32, 4], P('grp'), parts along dimension 0, may hold values from 0 to 3, as said below
- gate_probs: float32 [32, 4], P('grp'), parts along dimension 0, may hold values from 0.2 to 1
- w_gate: bfloat16 [4, 1536, 1536], P('kvp', None, 'tp'), may hold values from -0.15625 to 0.15625
- w_up: bfloat16 [4, 1536, 1536], P('kvp', None, 'tp'), may hold values from -0.15625 to 0.15625
- w_down: bfloat16 [4, 1536, 1536], P('kvp', 'tp'), may hold values from -0.15625 to 0.15625
Outputs:
- attended: float32 [32, 4096], P('grp', 'tp'), parts along dimension 0
- mixed: bfloat16 [32, 1536], P('grp', 'kvp'), parts along dimension 0
There are 2 independent parts, one for each index of `grp`. A program takes and returns all parts, laid end to end along the dimension named above; an argument that names none is the same for every part. Nothing has to cross between parts.
Inputs may be any that keep to these rules, and one draw needn't show every extreme that they name: `lengths`: at least one sequence has all 512 positions valid. `expert_ids`: each row names 4 different experts; no expert is named by more than 16 rows, and some expert by exactly 16.
All inputs are finite; a program needn't handle non-finite values.
Results may differ from a plain program's by a relative error of at most 0.006.
Values may be sent and summed in bfloat16 or wider, within the bound.
No kernel may reach another device: no remote copies, remote signals or barrier semaphores. Data moves between devices by JAX's collectives and lax.ppermute only.
A program may use at most 64 MiB of HBM per device.

v0:
```python
import jax
import jax.numpy as jnp
from jax import lax
from jax.sharding import PartitionSpec as P

D = 1536
HEAD = 64
EPSILON = 1e-05
NEGATIVE = -1e30


def merged(part, axis, combine):
    gathered = jax.tree.map(lambda a: lax.all_gather(a, axis), part)

    def take(source):
        return jax.tree.map(lambda a: lax.dynamic_index_in_dim(a, source, 0, False), gathered)

    return lax.fori_loop(
        1, lax.axis_size(axis), lambda source, state: combine(state, take(source)), take(0)
    )


def slot_tables(expert_ids, gate_probs, experts, capacity):
    batch_size, top_count = expert_ids.shape
    flat_ids = expert_ids.reshape(-1)
    pair_count = flat_ids.shape[0]
    pair_order = jnp.arange(pair_count, dtype=jnp.int32)
    earlier_same = (flat_ids[:, None] == flat_ids[None, :]) & (
        pair_order[None, :] < pair_order[:, None]
    )
    slot_index = jnp.sum(earlier_same.astype(jnp.int32), axis=1)
    target_col = flat_ids * capacity + slot_index
    columns = jnp.arange(experts * capacity, dtype=jnp.int32)
    hit_table = (target_col[:, None] == columns[None, :]).astype(jnp.float32)
    hit_table = hit_table.reshape(batch_size, top_count, experts * capacity)
    dispatch = jnp.sum(hit_table, axis=1)
    combine = jnp.sum(hit_table * gate_probs[:, :, None], axis=1)
    return (dispatch, combine)


def merge_partial(earlier, latest):
    global_max = jnp.maximum(earlier[0], latest[0])
    lead_scale = jnp.exp(earlier[0] - global_max)
    trail_scale = jnp.exp(latest[0] - global_max)
    return (
        global_max,
        lead_scale * earlier[1] + trail_scale * latest[1],
        lead_scale[..., None] * earlier[2] + trail_scale[..., None] * latest[2],
    )


def on_device(
    queries,
    keys,
    values,
    lengths,
    out_weight,
    residual,
    norm_gain,
    expert_ids,
    gate_probs,
    w_gate,
    w_up,
    w_down,
):
    batch_size = queries.shape[0]
    local_kv = keys.shape[2] // HEAD
    local_heads = queries.shape[1] // HEAD
    group_size = local_heads // local_kv
    ctx_dev = keys.shape[1]
    shards = lax.axis_size("kvp")
    query_heads = queries.reshape(batch_size, local_kv, group_size, HEAD)
    key_rows = keys.reshape(batch_size, ctx_dev, local_kv, HEAD)
    value_rows = values.reshape(batch_size, ctx_dev, local_kv, HEAD)
    scores = jnp.einsum(
        "bgrd,bcgd->bgrc", query_heads, key_rows, preferred_element_type=jnp.float32
    ) * HEAD ** (-0.5)
    position = lax.axis_index("kvp") * ctx_dev + jnp.arange(ctx_dev, dtype=jnp.int32)
    valid_key = (position[None, :] < lengths[:, None])[:, None, None, :]
    masked = jnp.where(valid_key, scores, NEGATIVE)
    block_max = jnp.max(masked, axis=3)
    weights = jnp.where(valid_key, jnp.exp(masked - block_max[..., None]), 0.0)
    rounded = weights.astype(jnp.bfloat16)
    block_sum = jnp.sum(rounded.astype(jnp.float32), axis=3)
    block_out = jnp.einsum(
        "bgrc,bcgd->bgrd", rounded, value_rows, preferred_element_type=jnp.float32
    )
    global_max, denominator, summed = merged(
        (block_max, block_sum, block_out), "kvp", merge_partial
    )
    attended = (summed / denominator[..., None]).reshape(batch_size, local_heads * HEAD)
    projected = lax.psum(
        jnp.dot(attended.astype(jnp.bfloat16), out_weight, preferred_element_type=jnp.float32), "tp"
    )
    hidden_state = lax.optimization_barrier(
        (projected + residual.astype(jnp.float32)).astype(jnp.bfloat16)
    )
    state_wide = hidden_state.astype(jnp.float32)
    col_count = hidden_state.shape[1]
    exp_dev = w_gate.shape[0]
    experts = exp_dev * shards
    capacity = min(batch_size, max(2, 2 * batch_size * expert_ids.shape[1] // experts))
    dispatch, combine = slot_tables(expert_ids, gate_probs, experts, capacity)
    total_sq = lax.psum(jnp.sum(state_wide * state_wide, axis=1), "kvp")
    inverse = lax.rsqrt(total_sq / D + EPSILON)
    normed = (state_wide * inverse[:, None] * norm_gain.astype(jnp.float32)[None, :]).astype(
        jnp.bfloat16
    )
    outgoing = jnp.dot(
        dispatch.T.astype(jnp.bfloat16), normed, preferred_element_type=jnp.float32
    ).astype(jnp.bfloat16)
    outgoing = outgoing.reshape(experts, capacity, col_count)
    expert_rows = lax.all_to_all(outgoing, "kvp", split_axis=0, concat_axis=2, tiled=True)
    gate_proj = jnp.einsum("ecd,edf->ecf", expert_rows, w_gate, preferred_element_type=jnp.float32)
    up_proj = jnp.einsum("ecd,edf->ecf", expert_rows, w_up, preferred_element_type=jnp.float32)
    activation = (jax.nn.silu(gate_proj) * up_proj).astype(jnp.bfloat16)
    partial_value = jnp.einsum(
        "ecf,efd->ecd", activation, w_down, preferred_element_type=jnp.float32
    )
    returned = lax.all_to_all(partial_value, "kvp", split_axis=2, concat_axis=0, tiled=True)
    moe_local = jnp.dot(
        combine, returned.reshape(experts * capacity, col_count), precision=lax.Precision.HIGHEST
    )
    moe_term = lax.psum(moe_local, "tp")
    mixed = (state_wide + moe_term).astype(jnp.bfloat16)
    return (attended, mixed)


def solution(mesh):
    return jax.shard_map(
        on_device,
        mesh=mesh,
        in_specs=(
            P("grp", "tp"),
            P("grp", "kvp", "tp"),
            P("grp", "kvp", "tp"),
            P("grp"),
            P("tp", "kvp"),
            P("grp", "kvp"),
            P("kvp"),
            P("grp", None),
            P("grp", None),
            P("kvp", None, "tp"),
            P("kvp", None, "tp"),
            P("kvp", "tp", None),
        ),
        out_specs=(P("grp", "tp"), P("grp", "kvp")),
        check_vma=False,
    )
```

profile of v0, /device:TPU:0, one launch (start us, length us, event | category | flops | bytes accessed | tf_op | source)
XLA Modules:
  0.0 124.9 jit_solution(10427162739778779653)
XLA Ops:
  0.6 0.0 copy-start
  0.6 0.0 copy-start.5
  0.7 0.8 convert_element_type.54
  1.4 0.8 copy.99
  2.2 0.1 eq.13
  2.3 0.2 convert_reduce_fusion.2
  2.5 0.1 reduce_sum.49
  2.6 0.1 copy.100
  2.6 1.3 %multiply_add_fusion = s32[16,4]{0,1:T(4,128)} fusion(s32[16,4]{0,1:T(4,128)S(1)} %copy.100, s32[16,4]{0,1:T(4,128)} %param.21), kind=kLoop, calls=%fused_computation.48 | loop fusion | flops 128 | bytes 768 | tf_op jit(solution)/shard_map/add | solution.py:32
  3.9 0.9 reshape.104
  4.8 0.0 copy-start.3
  4.8 1.4 %copy.90 = bf16[16,128,128]{1,2,0:T(8,128)(2,1)S(1)} copy(bf16[16,128,128]{2,1,0:T(8,128)(2,1)} %param.15) | data formatting | bytes 1048576 | tf_op args[1]
  6.2 0.0 copy-done.5
  6.2 0.1 broadcast_compare_fusion
  6.3 0.3 fusion.39
  6.6 14.9 %all-gather = f32[64,2,8]{2,1,0:T(2,128)S(1)} all-gather(f32[16,2,8]{2,1,0:T(2,128)S(1)} %get-tuple-element.236), channel_id=2, replica_groups=mesh['grp'=2,'kvp'=4,'tp'=4] {'kvp'}, dimensions={0}, use_global_device_ids=true | all-gather | bytes 5120 | tf_op jit(solution)/shard_map/all_gather | solution.py:13
  21.5 0.2 convert_reduce_fusion
  21.7 13.3 %all-gather.1 = f32[64,2,8]{2,1,0:T(2,128)S(1)} all-gather(f32[16,2,8]{2,1,0:T(2,128)S(1)} %convert_reduce_fusion), channel_id=3, replica_groups=mesh['grp'=2,'kvp'=4,'tp'=4] {'kvp'}, dimensions={0}, use_global_device_ids=true | all-gather | bytes 5120 | tf_op jit(solution)/shard_map/all_gather | solution.py:13
  35.1 0.1 copy.95
  35.1 0.1 copy.97
  35.2 0.1 copy.94
  35.3 0.1 copy.96
  35.4 0.0 copy-done.3
  35.4 0.3 copy.91
  35.7 0.4 fusion.35
  36.1 15.1 %all-gather.2 = f32[64,2,8,64]{3,2,1,0:T(8,128)S(1)} all-gather(f32[16,2,8,64]{3,2,1,0:T(8,128)S(1)} %fusion.35), channel_id=4, replica_groups=mesh['grp'=2,'kvp'=4,'tp'=4] {'kvp'}, dimensions={0}, use_global_device_ids=true | all-gather | bytes 327680 | tf_op jit(solution)/shard_map/all_gather | solution.py:13
  51.3 1.1 while.19
  51.3 0.1 copy.113
  51.4 0.1 copy.114
  51.5 0.2 fusion.53
  51.7 0.1 copy.113
  51.8 0.1 copy.114
  51.9 0.2 fusion.53
  52.1 0.1 copy.113
  52.2 0.1 copy.114
  52.2 0.2 fusion.53
  52.4 0.0 copy-start.2
  52.4 0.1 copy.98
  52.5 0.1 broadcast_divide_fusion
  52.6 0.7 reshape.107
  53.4 2.1 %fusion.18 = f32[16,384]{1,0:T(8,128)} fusion(bf16[1024,384]{1,0:T(8,128)(2,1)} %param.18, f32[16,1024]{1,0:T(8,128)} %reshape.107), kind=kOutput, calls=%fused_computation.30 | convolution fusion | flops 12599296 | bytes 876544 | tf_op jit(solution)/shard_map/dot_general | solution.py:93
  55.4 11.4 %psum.21 = f32[16,384]{1,0:T(8,128)} all-reduce(f32[16,384]{1,0:T(8,128)} %fusion.18), channel_id=1, replica_groups=mesh['grp'=2,'kvp'=4,'tp'=4] {'tp'}, use_global_device_ids=true, to_apply=%region_4.5 | all-reduce | flops 6144 | bytes 49152 | tf_op jit(solution)/shard_map/psum | solution.py:92
  66.8 0.7 add_convert_fusion
  67.5 0.6 fusion.21
  68.2 12.5 %psum.22 = f32[16]{0:T(128)} all-reduce(f32[16]{0:T(128)} %fusion.21), channel_id=1, replica_groups=mesh['grp'=2,'kvp'=4,'tp'=4] {'kvp'}, use_global_device_ids=true, to_apply=%region_9.10 | all-reduce | flops 16 | bytes 128 | tf_op jit(solution)/shard_map/psum | solution.py:104
  80.7 0.7 add_rsqrt_fusion
  81.4 1.4 %convert_reduce_fusion.1 = (bf16[16,64]{1,0:T(8,128)(2,1)S(1)}, f32[16,64]{1,0:T(8,128)}) fusion(s32[16,4]{0,1:T(4,128)} %multiply_add_fusion, f32[16,4]{0,1:T(4,128)} %param.22), kind=kLoop, calls=%fused_computation.25 | loop fusion | flops 18432 | bytes 6656 | tf_op jit(solution)/shard_map/reduce_sum | solution.py:36
  82.7 0.2 convolution_convert_fusion
  82.9 8.1 %all_to_all.30 = bf16[4,16,384]{2,1,0:T(8,128)(2,1)S(1)} all-to-all(bf16[4,16,384]{2,1,0:T(8,128)(2,1)S(1)} %bitcast.73), channel_id=1, replica_groups=mesh['grp'=2,'kvp'=4,'tp'=4] {'kvp'}, dimensions={0} | all-to-all | bytes 98304 | tf_op jit(solution)/shard_map/all_to_all | solution.py:113
  91.0 0.6 copy.110
  91.6 1.7 %fusion.7 = f32[16,384]{1,0:T(8,128)} fusion(bf16[16,1536]{1,0:T(8,128)(2,1)} %bitcast.23, bf16[1,1536,384]{2,1,0:T(8,128)(2,1)S(1)} %copy-done.2), kind=kOutput, calls=%fused_computation.12 | convolution fusion | flops 18874368 | bytes 1253376 | tf_op jit(solution)/shard_map/ecd,edf->ecf/dot_general | solution.py:114
  93.3 1.6 %fusion.3 = f32[16,1536]{0,1:T(8,128)S(1)} fusion(bf16[1,384,1536]{2,1,0:T(8,128)(2,1)S(1)} %copy-done, bf16[16,1536]{1,0:T(8,128)(2,1)} %bitcast.23, bf16[1,1536,384]{2,1,0:T(8,128)(2,1)S(1)} %copy-done.1, f32[16,384]{1,0:T(8,128)} %fusion.7), kind=kOutput, calls=%fused_computation.8 | convolution fusion | flops 37785600 | bytes 2531328 | tf_op jit(solution)/shard_map/ecf,efd->ecd/dot_general | solution.py:117
  95.0 0.6 broadcast.55
  95.6 7.2 %reduce = f32[1536,16]{1,0:T(8,128)S(1)} reduce(f32[1536,1,16]{2,1,0:T(1,128)S(1)} %bitcast.66, f32[]{:T(128)} %broadcast.55), dimensions={1}, to_apply=%bitcast.47.reduce_sub_computation | reduce | bytes 196612
  102.8 0.3 reshape.123
  103.1 0.0 copy-start.4
  103.1 8.2 %all_to_all.31 = f32[4,1,6144]{2,1,0:T(1,128)S(1)} all-to-all(f32[4,1,6144]{2,1,0:T(1,128)S(1)} %reshape.123), channel_id=1, replica_groups=mesh['grp'=2,'kvp'=4,'tp'=4] {'kvp'}, dimensions={0} | all-to-all | bytes 196608 | tf_op jit(solution)/shard_map/all_to_all | solution.py:120
  111.3 0.9 reduce.1
  112.3 1.3 %reshape.124 = f32[1536,1,16]{2,1,0:T(1,128)S(1)} reshape(f32[4,6144]{1,0:T(4,128)S(1)} %reduce.1) | data formatting | bytes 196608
  113.6 0.2 copy.109
  113.9 0.0 copy-done.4
  113.9 0.2 fusion.40
  114.0 10.3 %psum.23 = f32[16,384]{1,0:T(8,128)S(1)} all-reduce(f32[16,384]{1,0:T(8,128)S(1)} %fusion.40), channel_id=1, replica_groups=mesh['grp'=2,'kvp'=4,'tp'=4] {'tp'}, use_global_device_ids=true, to_apply=%region_10.11 | all-reduce | flops 6144 | bytes 49152 | tf_op jit(solution)/shard_map/psum | solution.py:124
  124.3 0.6 fusion.24
  (13 shorter events, 0.1 us)
Async XLA Ops:
  0.6 92.7 %copy-start = (bf16[1,384,1536]{2,1,0:T(8,128)(2,1)S(1)}, bf16[1,384,1536]{2,1,0:T(8,128)(2,1)}, u32[]{:S(2)}) copy-start(bf16[1,384,1536]{2,1,0:T(8,128)(2,1)} %param.25) | copy-start | bytes 3538948
  0.6 5.5 %copy-start.5 = (s32[16]{0:T(128)S(1)}, s32[16]{0:T(128)}, u32[]{:S(2)}) copy-start(s32[16]{0:T(128)} %param.17) | copy-start | bytes 196
  4.8 30.6 %copy-start.3 = (bf16[16,128,128]{2,1,0:T(8,128)(2,1)S(1)}, bf16[16,128,128]{2,1,0:T(8,128)(2,1)}, u32[]{:S(2)}) copy-start(bf16[16,128,128]{2,1,0:T(8,128)(2,1)} %param.16) | copy-start | bytes 1572868
  52.4 39.2 %copy-start.2 = (bf16[1,1536,384]{2,1,0:T(8,128)(2,1)S(1)}, bf16[1,1536,384]{2,1,0:T(8,128)(2,1)}, u32[]{:S(2)}) copy-start(bf16[1,1536,384]{2,1,0:T(8,128)(2,1)} %param.23) | copy-start | bytes 3538948
  53.4 40.0 %copy-start.1 = (bf16[1,1536,384]{2,1,0:T(8,128)(2,1)S(1)}, bf16[1,1536,384]{2,1,0:T(8,128)(2,1)}, u32[]{:S(2)}) copy-start(bf16[1,1536,384]{2,1,0:T(8,128)(2,1)} %param.24) | copy-start | bytes 3538948
  103.1 10.8 %copy-start.4 = (f32[16,64]{1,0:T(8,128)S(1)}, f32[16,64]{1,0:T(8,128)}, u32[]{:S(2)}) copy-start(f32[16,64]{1,0:T(8,128)} %get-tuple-element.217) | copy-start | bytes 12292
where the time goes:
time: 126 us; the launch traced here: 125 us
  blocking collectives  93.8 us (74%)
  other arithmetic  15.3 us (12%)
  local copies, waits for them, and re-layouts  8.31 us (7%)
  matrix products  6.53 us (5%)
    all_gather x3, blocking collectives, merged(): gathered = jax.tree.map(lambda a: lax.all_gather(a, axis), part)  43.4 us
    psum x1, blocking collectives, on_device(): total_sq = lax.psum(jnp.sum(state_wide * state_wide, axis=1), 'kvp')  12.5 us
    psum x1, blocking collectives, on_device(): lax.psum(jnp.dot(attended.astype(jnp.bfloat16), out_weight, preferred_ele...  11.4 us
    psum x1, blocking collectives, on_device(): moe_term = lax.psum(moe_local, 'tp')  10.3 us
    all_to_all x1, blocking collectives, on_device(): lax.all_to_all(partial_value, 'kvp', split_axis=2, concat_axis=0, tiled=T...  8.21 us
    all_to_all x1, blocking collectives, on_device(): lax.all_to_all(outgoing, 'kvp', split_axis=0, concat_axis=2, tiled=True)  8.06 us
    unnamed x1, other arithmetic  7.21 us
    unnamed x19, local copies, waits for them, and re-layouts  5.3 us

commit v1 on v0

--- a/solution.py
+++ b/solution.py
@@ -89,9 +89,9 @@
         (block_max, block_sum, block_out), "kvp", merge_partial
     )
     attended = (summed / denominator[..., None]).reshape(batch_size, local_heads * HEAD)
-    projected = lax.psum(
-        jnp.dot(attended.astype(jnp.bfloat16), out_weight, preferred_element_type=jnp.float32), "tp"
-    )
+    block = jnp.dot(attended.astype(jnp.bfloat16), out_weight, preferred_element_type=jnp.float32)
+    shards_2 = lax.all_gather(block, "tp")
+    projected = jnp.sum(shards_2, axis=0)
     hidden_state = lax.optimization_barrier(
         (projected + residual.astype(jnp.float32)).astype(jnp.bfloat16)
     )

time: 126 us -> 121 us (0.960)
  blocking collectives: 93.8 us -> 88.4 us
  other arithmetic: 15.3 us -> 16.9 us
    psum x1 -> x0, blocking collectives: 11.4 us -> none  [on_device(): lax.psum(jnp.dot(attended.astype(jnp.bfloat16), out_weight, preferred_ele...]
    all_gather x0 -> x1, blocking collectives: none -> 5.91 us  [on_device(): shards_2 = lax.all_gather(block, 'tp')]
    reduce_sum x0 -> x1, other arithmetic: none -> 1.51 us  [on_device(): projected = jnp.sum(shards_2, axis=0)]
    unnamed x19 -> x21, local copies, waits for them, and re-layouts: 5.3 us -> 5.92 us
where the time goes in v1:
time: 121 us; the launch traced here: 120 us
  blocking collectives  88.4 us (73%)
  other arithmetic  16.9 us (14%)
  local copies, waits for them, and re-layouts  8.31 us (7%)
  matrix products  5.77 us (5%)
    all_gather x3, blocking collectives, merged(): gathered = jax.tree.map(lambda a: lax.all_gather(a, axis), part)  43.4 us
    psum x1, blocking collectives, on_device(): total_sq = lax.psum(jnp.sum(state_wide * state_wide, axis=1), 'kvp')  12.5 us
    psum x1, blocking collectives, on_device(): moe_term = lax.psum(moe_local, 'tp')  10.3 us
    all_to_all x1, blocking collectives, on_device(): lax.all_to_all(partial_value, 'kvp', split_axis=2, concat_axis=0, tiled=T...  8.21 us
    all_to_all x1, blocking collectives, on_device(): lax.all_to_all(outgoing, 'kvp', split_axis=0, concat_axis=2, tiled=True)  8.06 us
    unnamed x1, other arithmetic  7.21 us
    unnamed x21, local copies, waits for them, and re-layouts  5.92 us
    all_gather x1, blocking collectives, on_device(): shards_2 = lax.all_gather(block, 'tp')  5.91 us

profile of v1, /device:TPU:0, one launch (start us, length us, event | category | flops | bytes accessed | tf_op | source)
XLA Modules:
  0.0 120.2 jit_solution(18288120567834153666)
XLA Ops:
  0.6 0.0 copy-start
  0.7 0.8 convert_element_type.54
  1.4 0.8 copy.99
  2.2 0.1 eq.13
  2.3 0.2 convert_reduce_fusion.2
  2.5 0.1 reduce_sum.59
  2.6 0.1 copy.100
  2.6 1.3 %multiply_add_fusion = s32[16,4]{0,1:T(4,128)} fusion(s32[16,4]{0,1:T(4,128)S(1)} %copy.100, s32[16,4]{0,1:T(4,128)} %param.21), kind=kLoop, calls=%fused_computation.48 | loop fusion | flops 128 | bytes 768 | tf_op jit(solution)/shard_map/add | solution.py:32
  3.9 0.9 reshape.104
  4.8 0.0 copy-start.3
  4.8 1.4 %copy.90 = bf16[16,128,128]{1,2,0:T(8,128)(2,1)S(1)} copy(bf16[16,128,128]{2,1,0:T(8,128)(2,1)} %param.15) | data formatting | bytes 1048576 | tf_op args[1]
  6.2 0.1 broadcast_compare_fusion
  6.3 0.3 fusion.39
  6.6 14.9 %all-gather = f32[64,2,8]{2,1,0:T(2,128)S(1)} all-gather(f32[16,2,8]{2,1,0:T(2,128)S(1)} %get-tuple-element.236), channel_id=2, replica_groups=mesh['grp'=2,'kvp'=4,'tp'=4] {'kvp'}, dimensions={0}, use_global_device_ids=true | all-gather | bytes 5120 | tf_op jit(solution)/shard_map/all_gather | solution.py:13
  21.5 0.2 convert_reduce_fusion
  21.8 13.3 %all-gather.1 = f32[64,2,8]{2,1,0:T(2,128)S(1)} all-gather(f32[16,2,8]{2,1,0:T(2,128)S(1)} %convert_reduce_fusion), channel_id=3, replica_groups=mesh['grp'=2,'kvp'=4,'tp'=4] {'kvp'}, dimensions={0}, use_global_device_ids=true | all-gather | bytes 5120 | tf_op jit(solution)/shard_map/all_gather | solution.py:13
  35.1 0.1 copy.95
  35.2 0.1 copy.97
  35.3 0.1 copy.94
  35.3 0.1 copy.96
  35.4 0.3 copy.91
  35.7 0.4 fusion.35
  36.2 15.1 %all-gather.2 = f32[64,2,8,64]{3,2,1,0:T(8,128)S(1)} all-gather(f32[16,2,8,64]{3,2,1,0:T(8,128)S(1)} %fusion.35), channel_id=4, replica_groups=mesh['grp'=2,'kvp'=4,'tp'=4] {'kvp'}, dimensions={0}, use_global_device_ids=true | all-gather | bytes 327680 | tf_op jit(solution)/shard_map/all_gather | solution.py:13
  51.3 1.1 while.19
  51.4 0.1 copy.113
  51.4 0.1 copy.114
  51.5 0.2 fusion.53
  51.7 0.1 copy.113
  51.8 0.1 copy.114
  51.9 0.2 fusion.53
  52.1 0.1 copy.113
  52.2 0.1 copy.114
  52.3 0.2 fusion.53
  52.5 0.0 copy-start.2
  52.5 0.1 copy.98
  52.5 0.1 broadcast_divide_fusion
  52.7 0.1 reshape.107
  52.8 0.6 copy-done.4
  53.4 1.3 %fusion.18 = f32[16,384]{1,0:T(8,128)S(1)} fusion(bf16[1024,384]{1,0:T(8,128)(2,1)} %param.18, f32[16,1024]{1,0:T(8,128)S(1)} %reshape.107), kind=kOutput, calls=%fused_computation.30 | convolution fusion | flops 12599296 | bytes 876544 | tf_op jit(solution)/shard_map/dot_general | solution.py:92
  54.7 0.0 copy-start.1
  54.7 5.9 %all-gather.3 = f32[64,384]{1,0:T(8,128)} all-gather(f32[16,384]{1,0:T(8,128)S(1)} %fusion.18), channel_id=5, replica_groups=mesh['grp'=2,'kvp'=4,'tp'=4] {'tp'}, dimensions={0}, use_global_device_ids=true | all-gather | bytes 122880 | tf_op jit(solution)/shard_map/all_gather | solution.py:93
  60.6 1.5 %reduce_sum.57 = f32[16,384]{1,0:T(8,128)} reduce(f32[4,16,384]{2,1,0:T(8,128)} %bitcast.72, f32[]{:T(128)} %constant.74.clone.1), dimensions={0}, to_apply=%region_4.5 | reduce | flops 18432 | bytes 122884 | tf_op jit(solution)/shard_map/reduce_sum | solution.py:94
  62.1 0.7 add_convert_fusion
  62.9 0.6 fusion.21
  63.5 12.5 %psum.14 = f32[16]{0:T(128)} all-reduce(f32[16]{0:T(128)} %fusion.21), channel_id=1, replica_groups=mesh['grp'=2,'kvp'=4,'tp'=4] {'kvp'}, use_global_device_ids=true, to_apply=%region_9.10 | all-reduce | flops 16 | bytes 128 | tf_op jit(solution)/shard_map/psum | solution.py:104
  76.0 0.7 add_rsqrt_fusion
  76.7 1.4 %convert_reduce_fusion.1 = (bf16[16,64]{1,0:T(8,128)(2,1)S(1)}, f32[16,64]{1,0:T(8,128)}) fusion(s32[16,4]{0,1:T(4,128)} %multiply_add_fusion, f32[16,4]{0,1:T(4,128)} %param.22), kind=kLoop, calls=%fused_computation.25 | loop fusion | flops 18432 | bytes 6656 | tf_op jit(solution)/shard_map/reduce_sum | solution.py:36
  78.1 0.2 convolution_convert_fusion
  78.3 8.1 %all_to_all.30 = bf16[4,16,384]{2,1,0:T(8,128)(2,1)S(1)} all-to-all(bf16[4,16,384]{2,1,0:T(8,128)(2,1)S(1)} %bitcast.75), channel_id=1, replica_groups=mesh['grp'=2,'kvp'=4,'tp'=4] {'kvp'}, dimensions={0} | all-to-all | bytes 98304 | tf_op jit(solution)/shard_map/all_to_all | solution.py:113
  86.4 0.6 copy.110
  87.0 1.7 %fusion.7 = f32[16,384]{1,0:T(8,128)} fusion(bf16[16,1536]{1,0:T(8,128)(2,1)} %bitcast.24, bf16[1,1536,384]{2,1,0:T(8,128)(2,1)S(1)} %copy-done.2), kind=kOutput, calls=%fused_computation.12 | convolution fusion | flops 18874368 | bytes 1253376 | tf_op jit(solution)/shard_map/ecd,edf->ecf/dot_general | solution.py:114
  88.7 0.0 copy-done.1
  88.7 1.6 %fusion.3 = f32[16,1536]{0,1:T(8,128)S(1)} fusion(bf16[1,384,1536]{2,1,0:T(8,128)(2,1)S(1)} %copy-done, bf16[16,1536]{1,0:T(8,128)(2,1)} %bitcast.24, bf16[1,1536,384]{2,1,0:T(8,128)(2,1)S(1)} %copy-done.1, f32[16,384]{1,0:T(8,128)} %fusion.7), kind=kOutput, calls=%fused_computation.8 | convolution fusion | flops 37785600 | bytes 2531328 | tf_op jit(solution)/shard_map/ecf,efd->ecd/dot_general | solution.py:117
  90.3 0.6 broadcast.55
  90.9 7.2 %reduce = f32[1536,16]{1,0:T(8,128)S(1)} reduce(f32[1536,1,16]{2,1,0:T(1,128)S(1)} %bitcast.67, f32[]{:T(128)} %broadcast.55), dimensions={1}, to_apply=%bitcast.48.reduce_sub_computation | reduce | bytes 196612
  98.1 0.3 reshape.124
  98.4 0.0 copy-start.5
  98.4 8.2 %all_to_all.31 = f32[4,1,6144]{2,1,0:T(1,128)S(1)} all-to-all(f32[4,1,6144]{2,1,0:T(1,128)S(1)} %reshape.124), channel_id=1, replica_groups=mesh['grp'=2,'kvp'=4,'tp'=4] {'kvp'}, dimensions={0} | all-to-all | bytes 196608 | tf_op jit(solution)/shard_map/all_to_all | solution.py:120
  106.7 0.9 reduce.1
  107.6 1.3 %reshape.125 = f32[1536,1,16]{2,1,0:T(1,128)S(1)} reshape(f32[4,6144]{1,0:T(4,128)S(1)} %reduce.1) | data formatting | bytes 196608
  108.9 0.2 copy.109
  109.2 0.2 fusion.40
  109.4 10.3 %psum.15 = f32[16,384]{1,0:T(8,128)S(1)} all-reduce(f32[16,384]{1,0:T(8,128)S(1)} %fusion.40), channel_id=1, replica_groups=mesh['grp'=2,'kvp'=4,'tp'=4] {'tp'}, use_global_device_ids=true, to_apply=%region_10.11 | all-reduce | flops 6144 | bytes 49152 | tf_op jit(solution)/shard_map/psum | solution.py:124
  119.6 0.6 fusion.24
  (16 shorter events, 0.1 us)
Async XLA Ops:
  0.6 88.1 %copy-start = (bf16[1,384,1536]{2,1,0:T(8,128)(2,1)S(1)}, bf16[1,384,1536]{2,1,0:T(8,128)(2,1)}, u32[]{:S(2)}) copy-start(bf16[1,384,1536]{2,1,0:T(8,128)(2,1)} %param.25) | copy-start | bytes 3538948
  0.6 5.6 %copy-start.6 = (s32[16]{0:T(128)S(1)}, s32[16]{0:T(128)}, u32[]{:S(2)}) copy-start(s32[16]{0:T(128)} %param.17) | copy-start | bytes 196
  4.8 30.6 %copy-start.3 = (bf16[16,128,128]{2,1,0:T(8,128)(2,1)S(1)}, bf16[16,128,128]{2,1,0:T(8,128)(2,1)}, u32[]{:S(2)}) copy-start(bf16[16,128,128]{2,1,0:T(8,128)(2,1)} %param.16) | copy-start | bytes 1572868
  52.5 34.5 %copy-start.2 = (bf16[1,1536,384]{2,1,0:T(8,128)(2,1)S(1)}, bf16[1,1536,384]{2,1,0:T(8,128)(2,1)}, u32[]{:S(2)}) copy-start(bf16[1,1536,384]{2,1,0:T(8,128)(2,1)} %param.23) | copy-start | bytes 3538948
  52.8 0.6 copy-start.4
  54.7 34.0 %copy-start.1 = (bf16[1,1536,384]{2,1,0:T(8,128)(2,1)S(1)}, bf16[1,1536,384]{2,1,0:T(8,128)(2,1)}, u32[]{:S(2)}) copy-start(bf16[1,1536,384]{2,1,0:T(8,128)(2,1)} %param.24) | copy-start | bytes 3538948
  98.4 10.8 %copy-start.5 = (f32[16,64]{1,0:T(8,128)S(1)}, f32[16,64]{1,0:T(8,128)}, u32[]{:S(2)}) copy-start(f32[16,64]{1,0:T(8,128)} %get-tuple-element.217) | copy-start | bytes 12292
